TPU v7x, 32 devices: a whole 2x2x4 slice. The times are simulated.
32 devices in a mesh: seq: 32 (over z, y, x, core).
Axes of the slice: x: 2, y: 2, z: 4, core: 2. Of those that a mesh axis runs over, the one named last changes fastest.
Arguments:
- history: float32 [12288, 1024], P('seq'), may hold values from -6 to 6
- taps: float32 [12288, 1024], P('seq'), may hold values from -0.109375 to 0.109375
- self_taps: float32 [1024, 256], P('seq'), may hold values from -0.375 to 0.375
- fresh: float32 [1024, 256], P('seq'), may hold values from -6 to 6
- gate: float32 [1024, 256], P('seq'), may hold values from -6 to 6
Outputs:
- gated: float32 [1024, 256], P('seq')
All inputs are finite; a program needn't handle non-finite values.
Results may differ from a plain program's by a relative error of at most 0.000053.
Values sent between devices are 32-bit elements; how exact they have to be, the bound alone decides.
A program may use at most 64 MiB of HBM per device.

v0:
```python
import math

import jax
import jax.numpy as jnp
import numpy as np
from jax import lax
from jax.experimental import pallas as pl
from jax.experimental.pallas import tpu as pltpu
from jax.sharding import PartitionSpec as P

AXIS = "seq"
AHEAD = 3
DIRECT = 3
PLANE = 8
MESH = pl.DeviceIdType.MESH
F32 = jnp.float32
BF16 = jnp.bfloat16


def dft_matrix(seg):
    phase = np.outer(4 * np.arange(seg) + 1, np.arange(seg)) % (4 * seg)
    angle = phase * (math.pi / (2 * seg))
    return np.concatenate([np.cos(angle), -np.sin(angle)], axis=0)


def halves(matrix):
    high = np.asarray(matrix, np.float32).astype(BF16)
    low = np.asarray(matrix - high.astype(np.float64), np.float32).astype(BF16)
    return high, low


def split(value):
    high = value.astype(BF16)
    return high, (value - high.astype(F32)).astype(BF16)


def mul_conj(a, b):
    return a[0] * b[0] + a[1] * b[1], a[1] * b[0] - a[0] * b[1]


def mul(a, b):
    return a[0] * b[0] - a[1] * b[1], a[0] * b[1] + a[1] * b[0]


def add(a, b):
    return a[0] + b[0], a[1] + b[1]


def turn(a):
    return -a[1], a[0]


def back(a):
    return a[1], -a[0]


def local_products(hs, ts):
    us = [None] + [add(ts[a], turn(ts[a - 1])) for a in range(1, len(ts))]
    first = mul_conj(hs[0], ts[0])
    for a in range(1, len(hs)):
        first = add(first, mul_conj(hs[a], us[a]))
    second = mul_conj(hs[1], ts[0])
    for a in range(2, len(hs)):
        second = add(second, mul_conj(hs[a], us[a - 1]))
    return first, second


def halo_products(first, second, h0, h1, t_near, t_before, h_after):
    one = mul_conj(h0, t_before)
    two = add(mul_conj(h1, t_before), mul_conj(h_after, t_near))
    return add(first, back(one)), add(add(second, one), back(two))


def own_products(f0, f1, s0, s1):
    first = mul(f0, s0)
    return first, add(turn(first), add(mul(f0, s1), mul(f1, s0)))


def plain_body(history, taps, self_taps, fresh, gate):
    n = lax.axis_size(AXIS)
    seg = fresh.shape[1] // 2
    matrix = jnp.asarray(dft_matrix(seg).astype(np.float32))
    hp = lax.Precision.HIGHEST
    before = lax.ppermute(taps[-seg:], AXIS, [(s, s + 1) for s in range(n - 1)])
    after = lax.ppermute(history[:seg], AXIS, [(s, s - 1) for s in range(1, n)])

    def forward(rows):
        spec = jnp.dot(matrix, rows, precision=hp)
        return spec[:seg], spec[seg:]

    def inverse(spec):
        return jnp.dot(matrix.T / seg, jnp.concatenate(spec, axis=0), precision=hp)

    count = history.shape[0] // seg
    hs = [forward(history[a * seg : (a + 1) * seg]) for a in range(count)]
    ts = [forward(taps[a * seg : (a + 1) * seg]) for a in range(count)]
    first, second = local_products(hs, ts)
    first, second = halo_products(first, second, hs[0], hs[1], ts[-2], forward(before), forward(after))
    part = jnp.concatenate([inverse(first), inverse(second)], axis=0).T
    summed = lax.psum_scatter(part, AXIS, scatter_dimension=0, tiled=True)
    f, s = fresh.T, self_taps.T
    own = own_products(forward(f[:seg]), forward(f[seg:]), forward(s[:seg]), forward(s[seg:]))
    own_part = jnp.concatenate([inverse(own[0]), inverse(own[1])], axis=0).T
    return gate * (summed + own_part)


def kernel(n, seg, hist, taps, self_taps_h, fresh_h, gate_h, fh_h, fl_h, gh_h, gl_h, out,
           self_taps, fresh, gate, fh, fl, gh, gl, hist_v, taps_v, tb, ha, sh0, sh1, st1, q0, q1, parts, d_recv, sums, y_send, y_recv, w_send, w_recv,
           p_recv, z_send, z_recv, x_send, x_recv,
           small_sem, load_sem, tb_s, tb_r, ha_s, ha_r, d_s, d_r, y_s, y_r, w_s, w_r,
           p_s, p_r, z_s, z_r, x_s, x_r):
    me = lax.axis_index(AXIS)
    nz = n // PLANE
    my_z, low = me // PLANE, me % PLANE
    core, x, y = me % 2, low // 2 % 2, low // 4
    rows = hist.shape[0]
    count = rows // seg
    width = hist.shape[1] // nz
    block = width // PLANE
    partner = me + 1 - 2 * core
    routed = nz - DIRECT
    last = nz - 1
    half = width // 2
    x_peer, y_peer = me + 2 - 4 * x, me + 4 - 8 * y
    diagonal = me + 2 - 4 * x + 4 - 8 * y
    near = (y_peer, diagonal, x_peer)

    def pieces(i, dev):
        base = ((dev // PLANE + 1 + i) % nz) * width
        if i < last:
            return [(pl.ds(pl.multiple_of(base, width), width), pl.ds(0, width))]
        row = dev % PLANE // 4
        return [
            (pl.ds(pl.multiple_of(base + ((row + 1 + h) % 2) * half, half), half), pl.ds(h * half, half))
            for h in range(2)
        ]

    def remote(src, dst, send, recv, dev):
        return pltpu.make_async_remote_copy(
            src_ref=src, dst_ref=dst, send_sem=send, recv_sem=recv, device_id=(dev,), device_id_type=MESH
        )

    has_next, has_prev = me < n - 1, me > 0
    outer = me + 2 * core - 1
    has_outer = (outer >= 0) & (outer < n)
    peers = [partner]
    peers += near
    peers += [(me + k * PLANE) % n for k in range(1, nz)]
    barrier = pltpu.get_barrier_semaphore()
    @pl.when(has_outer)
    def _():
        pl.semaphore_signal(barrier, inc=1, device_id=(outer,), device_id_type=MESH)

    for peer in peers:
        pl.semaphore_signal(barrier, inc=1, device_id=(peer,), device_id_type=MESH)

    small = [
        pltpu.make_async_copy(src, dst, small_sem.at[k])
        for k, (src, dst) in enumerate((
            (fh_h, fh), (fl_h, fl), (gh_h, gh), (gl_h, gl), (self_taps_h, self_taps), (fresh_h, fresh), (gate_h, gate),
        ))
    ]
    for copy in small:
        copy.start()
    loads = [[] for _ in range(nz)]
    for i in range(nz):
        for k, (src, dst) in enumerate(((hist, hist_v), (taps, taps_v))):
            for h, (here, there) in enumerate(pieces(i, me)):
                copy = pltpu.make_async_copy(src.at[:, here], dst.at[i, :, there], load_sem.at[k, i + h])
                copy.start()
                loads[i].append(copy)

    pl.semaphore_wait(barrier, len(peers) + jnp.where(has_outer, 1, 0))

    def taps_copies(i, dev):
        return [
            remote(taps.at[pl.ds(rows - seg, seg), here], tb.at[i, :, there], tb_s.at[i + h], tb_r.at[i + h], dev)
            for h, (here, there) in enumerate(pieces(i, dev))
        ]

    def hist_copies(i, dev):
        return [
            remote(hist.at[pl.ds(0, seg), here], ha.at[i, :, there], ha_s.at[i + h], ha_r.at[i + h], dev)
            for h, (here, there) in enumerate(pieces(i, dev))
        ]

    def send_halo(i):
        @pl.when(has_next)
        def _():
            for copy in taps_copies(i, me + 1):
                copy.start()

        @pl.when(has_prev)
        def _():
            for copy in hist_copies(i, me - 1):
                copy.start()

    for i in range(min(AHEAD, nz)):
        send_halo(i)

    def forward(value):
        both = jnp.concatenate(split(value), axis=0)
        spec = jnp.dot(fh[...], both, preferred_element_type=F32) + jnp.dot(
            fl[...], both, preferred_element_type=F32
        )
        return spec[:seg], spec[seg:]

    def keep(ref, i, spec):
        ref[i, :seg], ref[i, seg:] = spec

    def held(ref, i, at):
        return ref[i, :seg, at], ref[i, seg:, at]

    @pl.when(me == 0)
    def _():
        tb[...] = jnp.zeros_like(tb)

    @pl.when(me == n - 1)
    def _():
        ha[...] = jnp.zeros_like(ha)

    for copy in small:
        copy.wait()
    for i in range(nz):
        for copy in loads[i]:
            copy.wait()
        hs = [forward(hist_v[i, pl.ds(a * seg, seg)]) for a in range(count)]
        ts = [forward(taps_v[i, pl.ds(a * seg, seg)]) for a in range(count)]
        first, second = local_products(hs, ts)
        keep(sh0, i, hs[0])
        keep(sh1, i, hs[1])
        keep(st1, i, ts[-2])
        keep(q0, i, first)
        keep(q1, i, second)

    contract = (((1,), (1,)), ((), ()))

    def dot_t(a, b):
        return lax.dot_general(a, b, contract, preferred_element_type=F32)

    f, s = fresh[...], self_taps[...]
    both = jnp.concatenate(split(jnp.concatenate([f[:, :seg], f[:, seg:], s[:, :seg], s[:, seg:]], axis=0)), axis=1)
    spec = dot_t(both, fh[...]) + dot_t(both, fl[...])
    quads = [(spec[k * block : (k + 1) * block, :seg], spec[k * block : (k + 1) * block, seg:]) for k in range(4)]
    a, b = own_products(*quads)
    high, low_half = split(jnp.concatenate([jnp.concatenate(a, axis=1), jnp.concatenate(b, axis=1)], axis=0))
    res = dot_t(high, gh[...]) + dot_t(low_half, gh[...]) + dot_t(high, gl[...])
    own = jnp.concatenate([res[:block], res[block:]], axis=1)

    def inverse(spec):
        hi, lo = split(jnp.concatenate(spec, axis=0))
        return (
            jnp.dot(gh[...], hi, preferred_element_type=F32)
            + jnp.dot(gh[...], lo, preferred_element_type=F32)
            + jnp.dot(gl[...], hi, preferred_element_type=F32)
        ).T

    def chip_copy(i, h=None):
        span, k = (pl.ds(0, 4), i) if h is None else (pl.ds(2 * h, 2), i + h)
        return remote(parts.at[i, 1 - core, span], d_recv.at[i, span], d_s.at[k], d_r.at[k], partner)

    def y_copy(i):
        return remote(y_send.at[i], y_recv.at[i], y_s.at[i], y_r.at[i], y_peer)

    def w_copy(i):
        return remote(w_send.at[i], w_recv.at[i], w_s.at[i], w_r.at[i], (me + (i + 1) * PLANE) % n)

    def near_copy(i, j):
        k = i - routed
        return remote(sums.at[k, (0, 1, 3)[j]], p_recv.at[k, j], p_s.at[k, j], p_r.at[k, j], near[j])

    def z_copy(i):
        k = i - routed
        return remote(z_send.at[k], z_recv.at[k], z_s.at[k], z_r.at[k], (me + (i + 1) * PLANE) % n)

    def x_copy():
        return remote(x_send, x_recv, x_s, x_r, x_peer)

    def compute(i, h=None):
        which = slice(None) if h is None else slice(h, h + 1)

        @pl.when(has_prev)
        def _():
            for copy in taps_copies(i, me)[which]:
                copy.wait_recv()

        @pl.when(has_next)
        def _():
            for copy in hist_copies(i, me)[which]:
                copy.wait_recv()

        at = pl.ds(0, width) if h is None else pl.ds(h * half, half)
        both = halo_products(
            held(q0, i, at), held(q1, i, at), held(sh0, i, at), held(sh1, i, at), held(st1, i, at),
            forward(tb[i, :, at]), forward(ha[i, :, at]),
        )
        for side, spec in enumerate(both):
            res = inverse(spec)
            for k in range(res.shape[0] // block):
                col = k // 2 % 2
                row = (k // 4 + y + 1) % 2 if h is None else h
                place = 2 * row + (col + x) % 2
                parts[i, k % 2, place, :, pl.ds(side * seg, seg)] = res[k * block : (k + 1) * block]
        chip_copy(i, h).start()

    def route_y(i):
        chip_copy(i).wait_recv()
        y_send[i] = parts[i, core, :2] + d_recv[i, :2]
        y_copy(i).start()

    def route_z(i):
        y_copy(i).wait_recv()
        w_send[i] = parts[i, core, 2:] + d_recv[i, 2:] + y_recv[i]
        w_copy(i).start()

    def spread(i, h=None):
        chip_copy(i, h).wait_recv()
        lo, hi = (0, 4) if h is None else (2 * h, 2 * h + 2)
        sums[i - routed, lo:hi] = parts[i, core, lo:hi] + d_recv[i, lo:hi]
        for j, place in enumerate((0, 1, 3)):
            if lo <= place < hi:
                near_copy(i, j).start()

    def gathered(i):
        for j in range(3):
            near_copy(i, j).wait_recv()
        k = i - routed
        return sums[k, 2] + p_recv[k, 0] + p_recv[k, 1] + p_recv[k, 2]

    for i in range(last):
        compute(i)
        if i < routed:
            route_y(i)
        else:
            spread(i)
        if i + AHEAD < nz:
            send_halo(i + AHEAD)
        if 0 <= i - 1 < routed:
            route_z(i - 1)
    compute(last, 0)
    if routed == last:
        route_z(last - 1)
    spread(last, 0)
    compute(last, 1)
    spread(last, 1)
    for i in range(routed, last):
        z_send[i - routed] = gathered(i)
        z_copy(i).start()
    for i in range(routed):
        w_copy(i).wait_recv()
    total = gathered(last)
    if routed:
        merged = w_recv[0]
        for i in range(1, routed):
            merged = merged + w_recv[i]
        x_send[...] = merged[1]
        x_copy().start()
        total = total + merged[0]
    for i in range(routed, last):
        z_copy(i).wait_recv()
        total = total + z_recv[i - routed]
    if routed:
        x_copy().wait_recv()
        total = total + x_recv[...]
        x_copy().wait_send()
    out[...] = gate[...] * (total + own)

    for i in range(nz):
        @pl.when(has_next)
        def _(i=i):
            for copy in taps_copies(i, me + 1):
                copy.wait_send()

        @pl.when(has_prev)
        def _(i=i):
            for copy in hist_copies(i, me - 1):
                copy.wait_send()

        for h in (None,) if i < last else (0, 1):
            chip_copy(i, h).wait_send()
        if i < routed:
            y_copy(i).wait_send()
            w_copy(i).wait_send()
        else:
            for j in range(3):
                near_copy(i, j).wait_send()
            if i < last:
                z_copy(i).wait_send()


def kernel_body(history, taps, self_taps, fresh, gate):
    n = lax.axis_size(AXIS)
    rows, channels = history.shape
    block, new_len = fresh.shape
    seg = new_len // 2
    nz = n // PLANE
    width = channels // nz
    fh, fl = halves(dft_matrix(seg))
    gh, gl = halves(dft_matrix(seg).T / seg)
    fh, fl = np.concatenate([fh, fh], axis=1), np.concatenate([fl, fl], axis=1)
    vmem = pl.BlockSpec(memory_space=pltpu.VMEM)
    hbm = pl.BlockSpec(memory_space=pl.ANY)
    chips = PLANE // 2
    dma = pltpu.SemaphoreType.DMA
    spec = pltpu.VMEM((nz, 2 * seg, width), F32)
    pair = pltpu.VMEM((max(nz - DIRECT, 1), 2, block, new_len), F32)
    return pl.pallas_call(
        lambda *refs: kernel(n, seg, *refs),
        out_shape=pltpu.VMEM(fresh.shape, F32),
        in_specs=[hbm] * 9,
        out_specs=vmem,
        scratch_shapes=[
            pltpu.VMEM(fresh.shape, F32), pltpu.VMEM(fresh.shape, F32), pltpu.VMEM(fresh.shape, F32),
            pltpu.VMEM(fh.shape, BF16), pltpu.VMEM(fh.shape, BF16), pltpu.VMEM(gh.shape, BF16), pltpu.VMEM(gh.shape, BF16),
            pltpu.VMEM((nz, rows, width), F32),
            pltpu.VMEM((nz, rows, width), F32),
            pltpu.VMEM((nz, seg, width), F32),
            pltpu.VMEM((nz, seg, width), F32),
            spec, spec, spec, spec, spec,
            pltpu.VMEM((nz, 2, chips, block, new_len), F32),
            pltpu.VMEM((nz, chips, block, new_len), F32),
            pltpu.VMEM((DIRECT, chips, block, new_len), F32),
            pair, pair, pair, pair,
            pltpu.VMEM((DIRECT, 3, block, new_len), F32),
            pltpu.VMEM((DIRECT, block, new_len), F32),
            pltpu.VMEM((DIRECT, block, new_len), F32),
            pltpu.VMEM((block, new_len), F32),
            pltpu.VMEM((block, new_len), F32),
            dma((7,)),
            dma((2, nz + 1)),
            dma((nz + 1,)), dma((nz + 1,)), dma((nz + 1,)), dma((nz + 1,)),
            dma((nz + 1,)), dma((nz + 1,)),
            dma((nz,)), dma((nz,)), dma((nz,)), dma((nz,)),
            dma((DIRECT, 3)), dma((DIRECT, 3)),
            dma((DIRECT,)), dma((DIRECT,)),
            dma, dma,
        ],
        compiler_params=pltpu.CompilerParams(collective_id=0, has_side_effects=True),
        name="hyena",
    )(history, taps, self_taps, fresh, gate, *(jnp.asarray(m) for m in (fh, fl, gh, gl)))


def solution(mesh):
    n = mesh.shape[AXIS]

    def body(history, taps, self_taps, fresh, gate):
        channels = history.shape[1]
        block = fresh.shape[0]
        fits = n % PLANE == 0 and n >= DIRECT * PLANE and block % 8 == 0 and (block * PLANE) % 256 == 0
        chosen = kernel_body if fits and channels == block * n else plain_body
        return chosen(history, taps, self_taps, fresh, gate)

    spec = P(AXIS, None)
    return jax.shard_map(body, mesh=mesh, in_specs=(spec,) * 5, out_specs=spec, check_vma=False)
```

profile of v0, /device:TPU:0, one launch (start us, length us, event | category | flops | bytes accessed | tf_op | source)
XLA Modules:
  0.0 29.2 jit_solution(3834305089269969572)
XLA Ops:
  0.0 28.6 %hyena.1 = f32[32,256]{1,0:T(8,128)S(1)} custom-call(f32[384,1024]{1,0:T(8,128)} %refs_0_.1, f32[384,1024]{1,0:T(8,128)} %refs_1_.1, f32[32,256]{1,0:T(8,128)} %refs_2_.1, f32[32,256]{1,0:T(8,128)} %refs_3_.1, f32[32,256]{1,0:T(8,128)} %refs_4_.1, bf16[256,256]{1,0:T(8,128)(2,1)} %constant.8.clone.refs_5_, bf16[256,256]{1,0:T(8,128)(2,1)} %constant.9.clone.refs_6_, ...), custom_call_target="tpu_custom_call" | custom-call | tf_op jit(solution)/shard_map/hyena/pallas_call | solution.py:407
  28.6 0.6 %copy.11 = f32[32,256]{1,0:T(8,128)} copy(f32[32,256]{1,0:T(8,128)S(1)} %hyena.1) | data formatting | bytes 65536
where the time goes:
time: 29.3 us; the launch traced here: 29.2 us
  Pallas kernels  28.6 us (98%)
  local copies, waits for them, and re-layouts  0.62 us (2%)
    pallas_call x1, Pallas kernels, kernel_body(): pl.pallas_call(lambda *refs: kernel(n, seg, *refs), out_shape=pltpu.VMEM(...  28.6 us
    unnamed x1, local copies, waits for them, and re-layouts  0.62 us

commit v1 on v0

v1 whole, which is shorter than its diff:
```python
import math

import jax
import jax.numpy as jnp
import numpy as np
from jax import lax
from jax.experimental import pallas as pl
from jax.experimental.pallas import tpu as pltpu
from jax.sharding import PartitionSpec as P

AXIS = "seq"
PLANE = 8
MESH = pl.DeviceIdType.MESH
F32 = jnp.float32
BF16 = jnp.bfloat16
scope = jax.named_scope
AHEAD = 3


def dft_matrix(seg):
    phase = np.outer(4 * np.arange(seg) + 1, np.arange(seg)) % (4 * seg)
    angle = phase * (math.pi / (2 * seg))
    return np.concatenate([np.cos(angle), -np.sin(angle)], axis=0)


def halves(matrix):
    high = np.asarray(matrix, np.float32).astype(BF16)
    low = np.asarray(matrix - high.astype(np.float64), np.float32).astype(BF16)
    return high, low


def split(value):
    high = value.astype(BF16)
    return high, (value - high.astype(F32)).astype(BF16)


def mul_conj(a, b):
    return a[0] * b[0] + a[1] * b[1], a[1] * b[0] - a[0] * b[1]


def mul(a, b):
    return a[0] * b[0] - a[1] * b[1], a[0] * b[1] + a[1] * b[0]


def add(a, b):
    return a[0] + b[0], a[1] + b[1]


def turn(a):
    return -a[1], a[0]


def back(a):
    return a[1], -a[0]


def local_products(hs, ts):
    us = [None] + [add(ts[a], turn(ts[a - 1])) for a in range(1, len(ts))]
    first = mul_conj(hs[0], ts[0])
    for a in range(1, len(hs)):
        first = add(first, mul_conj(hs[a], us[a]))
    second = mul_conj(hs[1], ts[0])
    for a in range(2, len(hs)):
        second = add(second, mul_conj(hs[a], us[a - 1]))
    return first, second


def halo_products(first, second, h0, h1, t_near, t_before, h_after):
    one = mul_conj(h0, t_before)
    two = add(mul_conj(h1, t_before), mul_conj(h_after, t_near))
    return add(first, back(one)), add(add(second, one), back(two))


def own_products(f0, f1, s0, s1):
    first = mul(f0, s0)
    return first, add(turn(first), add(mul(f0, s1), mul(f1, s0)))


def plain_body(history, taps, self_taps, fresh, gate):
    n = lax.axis_size(AXIS)
    seg = fresh.shape[1] // 2
    matrix = jnp.asarray(dft_matrix(seg).astype(np.float32))
    hp = lax.Precision.HIGHEST
    before = lax.ppermute(taps[-seg:], AXIS, [(s, s + 1) for s in range(n - 1)])
    after = lax.ppermute(history[:seg], AXIS, [(s, s - 1) for s in range(1, n)])

    def forward(rows):
        spec = jnp.dot(matrix, rows, precision=hp)
        return spec[:seg], spec[seg:]

    def inverse(spec):
        return jnp.dot(matrix.T / seg, jnp.concatenate(spec, axis=0), precision=hp)

    count = history.shape[0] // seg
    hs = [forward(history[a * seg : (a + 1) * seg]) for a in range(count)]
    ts = [forward(taps[a * seg : (a + 1) * seg]) for a in range(count)]
    first, second = local_products(hs, ts)
    first, second = halo_products(first, second, hs[0], hs[1], ts[-2], forward(before), forward(after))
    part = jnp.concatenate([inverse(first), inverse(second)], axis=0).T
    summed = lax.psum_scatter(part, AXIS, scatter_dimension=0, tiled=True)
    f, s = fresh.T, self_taps.T
    own = own_products(forward(f[:seg]), forward(f[seg:]), forward(s[:seg]), forward(s[seg:]))
    own_part = jnp.concatenate([inverse(own[0]), inverse(own[1])], axis=0).T
    return gate * (summed + own_part)


def flip(z, mask):
    value, bit = z, 1
    while bit <= mask:
        if mask & bit:
            value = value + bit - 2 * bit * (z // bit % 2)
        bit *= 2
    return value


def kernel(n, seg, hist, taps, self_taps_h, fresh_h, gate_h, fh_h, fl_h, gh_h, gl_h, out,
           self_taps, fresh, gate, fh, fl, gh, gl, hist_v, taps_v, tb, ha, sh0, sh1, st1, q0, q1,
           parts, d_recv, y_send, y_recv, w_send, w_recv, v_send, v_recv, sums, n_recv,
           small_sem, load_sem, tb_s, tb_r, ha_s, ha_r, d_s, d_r, y_s, y_r, w_s, w_r, v_s, v_r, n_s, n_r):
    me = lax.axis_index(AXIS)
    nz = n // PLANE
    my_z, low = me // PLANE, me % PLANE
    core, x, y = me % 2, low // 2 % 2, low // 4
    rows = hist.shape[0]
    count = rows // seg
    width = hist.shape[1] // nz
    half = width // 2
    block = width // PLANE
    last = nz - 1
    far = nz - 2
    partner = me + 1 - 2 * core
    x_peer, y_peer = me + 2 - 4 * x, me + 4 - 8 * y
    diagonal = me + 2 - 4 * x + 4 - 8 * y
    near = (y_peer, diagonal, x_peer)
    steps = [(0, 0), (1, 0), (2, 0), (0, 1), (1, 1), (2, 1), (3, 0), (3, 1)]

    def level(i):
        return me + (flip(my_z, last - i) - my_z) * PLANE

    def cols(i, h, dev):
        row = dev % PLANE // 4
        base = flip(dev // PLANE, last - i) * width + ((row + 1 + h) % 2) * half
        return pl.ds(pl.multiple_of(base, half), half)

    def lanes(h):
        return pl.ds(h * half, half)

    def remote(src, dst, send, recv, dev):
        return pltpu.make_async_remote_copy(
            src_ref=src, dst_ref=dst, send_sem=send, recv_sem=recv, device_id=(dev,), device_id_type=MESH
        )

    has_next, has_prev = me < n - 1, me > 0
    outer = me + 2 * core - 1
    has_outer = (outer >= 0) & (outer < n)
    peers = [partner]
    peers += near
    peers += [level(i) + j * (2 - 4 * x) for i in range(last) for j in range(2)]
    barrier = pltpu.get_barrier_semaphore()
    @pl.when(has_outer)
    def _():
        pl.semaphore_signal(barrier, inc=1, device_id=(outer,), device_id_type=MESH)

    for peer in peers:
        pl.semaphore_signal(barrier, inc=1, device_id=(peer,), device_id_type=MESH)

    small = [
        pltpu.make_async_copy(src, dst, small_sem.at[k])
        for k, (src, dst) in enumerate((
            (fh_h, fh), (fl_h, fl), (gh_h, gh), (gl_h, gl), (self_taps_h, self_taps), (fresh_h, fresh), (gate_h, gate),
        ))
    ]
    for copy in small:
        copy.start()
    loads = [[] for _ in range(nz)]
    for i, h in steps:
        for k, (src, dst) in enumerate(((hist, hist_v), (taps, taps_v))):
            copy = pltpu.make_async_copy(src.at[:, cols(i, h, me)], dst.at[i, :, lanes(h)], load_sem.at[k, 2 * i + h])
            copy.start()
            loads[i].append(copy)

    with scope("barrier"):
        pl.semaphore_wait(barrier, len(peers) + jnp.where(has_outer, 1, 0))

    def taps_copy(i, h, dev):
        k = 2 * i + h
        return remote(
            taps.at[pl.ds(rows - seg, seg), cols(i, h, dev)], tb.at[i, :, lanes(h)], tb_s.at[k], tb_r.at[k], dev
        )

    def hist_copy(i, h, dev):
        k = 2 * i + h
        return remote(hist.at[pl.ds(0, seg), cols(i, h, dev)], ha.at[i, :, lanes(h)], ha_s.at[k], ha_r.at[k], dev)

    up = has_next & (low == PLANE - 1)
    down = has_prev & (low == 0)

    def send_halo(k, forward_when, back_when):
        i, h = steps[k]

        @pl.when(forward_when)
        def _():
            taps_copy(i, h, me + 1).start()

        @pl.when(back_when)
        def _():
            hist_copy(i, h, me - 1).start()

    for k in range(len(steps)):
        if k < AHEAD:
            send_halo(k, has_next, has_prev)
        else:
            send_halo(k, has_next & ~up, has_prev & ~down)

    def forward(value):
        both = jnp.concatenate(split(value), axis=0)
        spec = jnp.dot(fh[...], both, preferred_element_type=F32) + jnp.dot(
            fl[...], both, preferred_element_type=F32
        )
        return spec[:seg], spec[seg:]

    def keep(ref, i, spec):
        ref[i, :seg], ref[i, seg:] = spec

    def held(ref, i, at):
        return ref[i, :seg, at], ref[i, seg:, at]

    @pl.when(me == 0)
    def _():
        tb[...] = jnp.zeros_like(tb)

    @pl.when(me == n - 1)
    def _():
        ha[...] = jnp.zeros_like(ha)

    for copy in small:
        copy.wait()
    for i in range(nz):
        for copy in loads[i]:
            copy.wait()
        with scope(f"local{i}"):
            hs = [forward(hist_v[i, pl.ds(a * seg, seg)]) for a in range(count)]
            ts = [forward(taps_v[i, pl.ds(a * seg, seg)]) for a in range(count)]
            first, second = local_products(hs, ts)
            keep(sh0, i, hs[0])
            keep(sh1, i, hs[1])
            keep(st1, i, ts[-2])
            keep(q0, i, first)
            keep(q1, i, second)

    contract = (((1,), (1,)), ((), ()))

    def dot_t(a, b):
        return lax.dot_general(a, b, contract, preferred_element_type=F32)

    def own_part():
        f, s = fresh[...], self_taps[...]
        both = jnp.concatenate(
            split(jnp.concatenate([f[:, :seg], f[:, seg:], s[:, :seg], s[:, seg:]], axis=0)), axis=1
        )
        spec = dot_t(both, fh[...]) + dot_t(both, fl[...])
        quads = [
            (spec[k * block : (k + 1) * block, :seg], spec[k * block : (k + 1) * block, seg:]) for k in range(4)
        ]
        a, b = own_products(*quads)
        high, low_half = split(
            jnp.concatenate([jnp.concatenate(a, axis=1), jnp.concatenate(b, axis=1)], axis=0)
        )
        res = dot_t(high, gh[...]) + dot_t(low_half, gh[...]) + dot_t(high, gl[...])
        return jnp.concatenate([res[:block], res[block:]], axis=1)

    def inverse(spec):
        hi, lo = split(jnp.concatenate(spec, axis=0))
        return (
            jnp.dot(gh[...], hi, preferred_element_type=F32)
            + jnp.dot(gh[...], lo, preferred_element_type=F32)
            + jnp.dot(gl[...], hi, preferred_element_type=F32)
        ).T

    def chip_copy(i, h):
        k = 2 * i + h
        return remote(parts.at[k, 1 - core], d_recv.at[k], d_s.at[k], d_r.at[k], partner)

    def y_copy(i):
        return remote(y_send.at[i], y_recv.at[i], y_s.at[i], y_r.at[i], y_peer)

    def w_copy(i, j):
        dev = level(i) + j * (2 - 4 * x)
        place = x + j * (1 - 2 * x)
        return remote(w_send.at[i, place], w_recv.at[i, j], w_s.at[i, j], w_r.at[i, j], dev)

    def v_copy():
        return remote(v_send, v_recv, v_s, v_r, level(far))

    def near_copy(j):
        src = sums.at[0, x] if j == 0 else sums.at[j - 1, 1 - x]
        return remote(src, n_recv.at[j], n_s.at[j], n_r.at[j], near[j])

    def compute(i, h):
        with scope(f"halo{i}{h}"):
            @pl.when(has_prev)
            def _():
                taps_copy(i, h, me).wait_recv()

            @pl.when(has_next)
            def _():
                hist_copy(i, h, me).wait_recv()

        at_step = steps.index((i, h))
        if at_step + AHEAD < len(steps):
            send_halo(at_step + AHEAD, up, down)

        with scope(f"comp{i}{h}"):
            at = lanes(h)
            both = halo_products(
                held(q0, i, at), held(q1, i, at), held(sh0, i, at), held(sh1, i, at), held(st1, i, at),
                forward(tb[i, :, at]), forward(ha[i, :, at]),
            )
            for side, spec in enumerate(both):
                res = inverse(spec)
                for k in range(res.shape[0] // block):
                    parts[2 * i + h, k % 2, k // 2, :, pl.ds(side * seg, seg)] = res[k * block : (k + 1) * block]
            chip_copy(i, h).start()

    def chip_sum(i, h):
        with scope(f"chip{i}{h}"):
            chip_copy(i, h).wait_recv()
        return parts[2 * i + h, core] + d_recv[2 * i + h]

    def route_y(i):
        y_send[i] = chip_sum(i, 0)
        y_copy(i).start()

    def route_w(i):
        value = chip_sum(i, 1)
        with scope(f"y{i}"):
            y_copy(i).wait_recv()
        w_send[i] = value + y_recv[i]
        for j in (1, 0):
            w_copy(i, j).start()

    def route_v(h):
        if h == 0:
            v_send[...] = chip_sum(far, 0)
            v_copy().start()
        else:
            w_send[far] = chip_sum(far, 1)
            for j in (1, 0):
                w_copy(far, j).start()

    own = own_part()
    compute(0, 0)
    compute(1, 0)
    route_y(0)
    compute(2, 0)
    route_y(1)
    compute(0, 1)
    route_v(0)
    compute(1, 1)
    route_w(0)
    compute(2, 1)
    route_w(1)
    compute(3, 0)
    route_v(1)
    compute(3, 1)
    first = chip_sum(last, 0)
    with scope("v0"):
        v_copy().wait_recv()
    sums[0] = first + v_recv[...]
    near_copy(0).start()
    near_copy(1).start()
    second = chip_sum(last, 1)
    sums[1] = second
    near_copy(2).start()
    total = sums[1, x] + own
    for j in range(3):
        with scope(f"near{j}"):
            near_copy(j).wait_recv()
        total = total + n_recv[j]
    for i in range(far + 1):
        for j in range(2):
            with scope(f"w{i}{j}"):
                w_copy(i, j).wait_recv()
            total = total + w_recv[i, j]
    out[...] = gate[...] * total

    with scope("sends"):
        for i, h in steps:
            @pl.when(has_next)
            def _(i=i, h=h):
                taps_copy(i, h, me + 1).wait_send()

            @pl.when(has_prev)
            def _(i=i, h=h):
                hist_copy(i, h, me - 1).wait_send()

            chip_copy(i, h).wait_send()
        for i in range(far):
            y_copy(i).wait_send()
        for i in range(far + 1):
            for j in range(2):
                w_copy(i, j).wait_send()
        v_copy().wait_send()
        for j in range(3):
            near_copy(j).wait_send()


def kernel_body(history, taps, self_taps, fresh, gate):
    n = lax.axis_size(AXIS)
    rows, channels = history.shape
    block, new_len = fresh.shape
    seg = new_len // 2
    nz = n // PLANE
    width = channels // nz
    fh, fl = halves(dft_matrix(seg))
    gh, gl = halves(dft_matrix(seg).T / seg)
    fh, fl = np.concatenate([fh, fh], axis=1), np.concatenate([fl, fl], axis=1)
    vmem = pl.BlockSpec(memory_space=pltpu.VMEM)
    hbm = pl.BlockSpec(memory_space=pl.ANY)
    dma = pltpu.SemaphoreType.DMA
    spec = pltpu.VMEM((nz, 2 * seg, width), F32)
    far = nz - 2

    def pairs(*lead):
        return pltpu.VMEM((*lead, 2, block, new_len), F32)

    return pl.pallas_call(
        lambda *refs: kernel(n, seg, *refs),
        out_shape=pltpu.VMEM(fresh.shape, F32),
        in_specs=[hbm] * 9,
        out_specs=vmem,
        scratch_shapes=[
            pltpu.VMEM(fresh.shape, F32), pltpu.VMEM(fresh.shape, F32), pltpu.VMEM(fresh.shape, F32),
            pltpu.VMEM(fh.shape, BF16), pltpu.VMEM(fh.shape, BF16), pltpu.VMEM(gh.shape, BF16), pltpu.VMEM(gh.shape, BF16),
            pltpu.VMEM((nz, rows, width), F32),
            pltpu.VMEM((nz, rows, width), F32),
            pltpu.VMEM((nz, seg, width), F32),
            pltpu.VMEM((nz, seg, width), F32),
            spec, spec, spec, spec, spec,
            pairs(2 * nz, 2), pairs(2 * nz),
            pairs(far), pairs(far), pairs(far + 1), pairs(far + 1),
            pairs(), pairs(),
            pairs(2),
            pltpu.VMEM((3, block, new_len), F32),
            dma((7,)),
            dma((2, 2 * nz)),
            dma((2 * nz,)), dma((2 * nz,)), dma((2 * nz,)), dma((2 * nz,)),
            dma((2 * nz,)), dma((2 * nz,)),
            dma((far,)), dma((far,)), dma((far + 1, 2)), dma((far + 1, 2)),
            dma, dma,
            dma((3,)), dma((3,)),
        ],
        compiler_params=pltpu.CompilerParams(collective_id=0, has_side_effects=True),
        name="hyena",
    )(history, taps, self_taps, fresh, gate, *(jnp.asarray(m) for m in (fh, fl, gh, gl)))


def solution(mesh):
    n = mesh.shape[AXIS]

    def body(history, taps, self_taps, fresh, gate):
        channels = history.shape[1]
        block = fresh.shape[0]
        planes = n // PLANE
        fits = n % PLANE == 0 and planes >= 4 and planes & (planes - 1) == 0 and block % 32 == 0
        chosen = kernel_body if fits and channels == block * n else plain_body
        return chosen(history, taps, self_taps, fresh, gate)

    spec = P(AXIS, None)
    return jax.shard_map(body, mesh=mesh, in_specs=(spec,) * 5, out_specs=spec, check_vma=False)
```

time: 29.3 us -> 26.2 us (0.89)
  Pallas kernels: 28.6 us -> 25.5 us
    pallas_call x1, Pallas kernels: 28.6 us -> 25.5 us  [kernel_body(): pl.pallas_call(lambda *refs: kernel(n, seg, *refs), out_shape=pltpu.VMEM(...]
where the time goes in v1:
time: 26.2 us; the launch traced here: 26.1 us
  Pallas kernels  25.5 us (97%)
  local copies, waits for them, and re-layouts  0.62 us (2%)
    pallas_call x1, Pallas kernels, kernel_body(): pl.pallas_call(lambda *refs: kernel(n, seg, *refs), out_shape=pltpu.VMEM(...  25.5 us
    unnamed x1, local copies, waits for them, and re-layouts  0.62 us

profile of v1, /device:TPU:0, one launch (start us, length us, event | category | flops | bytes accessed | tf_op | source)
XLA Modules:
  0.0 26.1 jit_solution(6432688634389579132)
XLA Ops:
  0.0 25.5 %hyena.1 = f32[32,256]{1,0:T(8,128)S(1)} custom-call(f32[384,1024]{1,0:T(8,128)} %refs_0_.1, f32[384,1024]{1,0:T(8,128)} %refs_1_.1, f32[32,256]{1,0:T(8,128)} %refs_2_.1, f32[32,256]{1,0:T(8,128)} %refs_3_.1, f32[32,256]{1,0:T(8,128)} %refs_4_.1, bf16[256,256]{1,0:T(8,128)(2,1)} %constant.8.clone.refs_5_, bf16[256,256]{1,0:T(8,128)(2,1)} %constant.9.clone.refs_6_, ...), custom_call_target="tpu_custom_call" | custom-call | tf_op jit(solution)/shard_map/hyena/pallas_call | solution.py:427
  25.5 0.6 %copy.11 = f32[32,256]{1,0:T(8,128)} copy(f32[32,256]{1,0:T(8,128)S(1)} %hyena.1) | data formatting | bytes 65536

commit v2 on v1

v2 whole, which is shorter than its diff:
```python
import math

import jax
import jax.numpy as jnp
import numpy as np
from jax import lax
from jax.experimental import pallas as pl
from jax.experimental.pallas import tpu as pltpu
from jax.sharding import PartitionSpec as P

AXIS = "seq"
PLANE = 8
MESH = pl.DeviceIdType.MESH
F32 = jnp.float32
BF16 = jnp.bfloat16
scope = jax.named_scope
AHEAD = 3


def dft_matrix(seg):
    phase = np.outer(4 * np.arange(seg) + 1, np.arange(seg)) % (4 * seg)
    angle = phase * (math.pi / (2 * seg))
    return np.concatenate([np.cos(angle), -np.sin(angle)], axis=0)


def halves(matrix):
    high = np.asarray(matrix, np.float32).astype(BF16)
    low = np.asarray(matrix - high.astype(np.float64), np.float32).astype(BF16)
    return high, low


def split(value):
    high = value.astype(BF16)
    return high, (value - high.astype(F32)).astype(BF16)


def mul_conj(a, b):
    return a[0] * b[0] + a[1] * b[1], a[1] * b[0] - a[0] * b[1]


def mul(a, b):
    return a[0] * b[0] - a[1] * b[1], a[0] * b[1] + a[1] * b[0]


def add(a, b):
    return a[0] + b[0], a[1] + b[1]


def turn(a):
    return -a[1], a[0]


def back(a):
    return a[1], -a[0]


def local_products(hs, ts):
    us = [None] + [add(ts[a], turn(ts[a - 1])) for a in range(1, len(ts))]
    first = mul_conj(hs[0], ts[0])
    for a in range(1, len(hs)):
        first = add(first, mul_conj(hs[a], us[a]))
    second = mul_conj(hs[1], ts[0])
    for a in range(2, len(hs)):
        second = add(second, mul_conj(hs[a], us[a - 1]))
    return first, second


def halo_products(first, second, h0, h1, t_near, t_before, h_after):
    one = mul_conj(h0, t_before)
    two = add(mul_conj(h1, t_before), mul_conj(h_after, t_near))
    return add(first, back(one)), add(add(second, one), back(two))


def own_products(f0, f1, s0, s1):
    first = mul(f0, s0)
    return first, add(turn(first), add(mul(f0, s1), mul(f1, s0)))


def plain_body(history, taps, self_taps, fresh, gate):
    n = lax.axis_size(AXIS)
    seg = fresh.shape[1] // 2
    matrix = jnp.asarray(dft_matrix(seg).astype(np.float32))
    hp = lax.Precision.HIGHEST
    before = lax.ppermute(taps[-seg:], AXIS, [(s, s + 1) for s in range(n - 1)])
    after = lax.ppermute(history[:seg], AXIS, [(s, s - 1) for s in range(1, n)])

    def forward(rows):
        spec = jnp.dot(matrix, rows, precision=hp)
        return spec[:seg], spec[seg:]

    def inverse(spec):
        return jnp.dot(matrix.T / seg, jnp.concatenate(spec, axis=0), precision=hp)

    count = history.shape[0] // seg
    hs = [forward(history[a * seg : (a + 1) * seg]) for a in range(count)]
    ts = [forward(taps[a * seg : (a + 1) * seg]) for a in range(count)]
    first, second = local_products(hs, ts)
    first, second = halo_products(first, second, hs[0], hs[1], ts[-2], forward(before), forward(after))
    part = jnp.concatenate([inverse(first), inverse(second)], axis=0).T
    summed = lax.psum_scatter(part, AXIS, scatter_dimension=0, tiled=True)
    f, s = fresh.T, self_taps.T
    own = own_products(forward(f[:seg]), forward(f[seg:]), forward(s[:seg]), forward(s[seg:]))
    own_part = jnp.concatenate([inverse(own[0]), inverse(own[1])], axis=0).T
    return gate * (summed + own_part)


def flip(z, mask):
    value, bit = z, 1
    while bit <= mask:
        if mask & bit:
            value = value + bit - 2 * bit * (z // bit % 2)
        bit *= 2
    return value


def kernel(n, seg, hist, taps, self_taps_h, fresh_h, gate_h, tables_h, out,
           rows_v, tables, both_v, halo_v, sh0, sh1, st1, q0, q1,
           parts, d_recv, y_send, y_recv, w_send, v_send, v_recv, sums, final,
           ready, small_sem, load_sem, t_s, h_s, halo_r, d_s, d_r, y_s, y_r, w_s, v_s, v_r, n_s, final_r):
    me = lax.axis_index(AXIS)
    nz = n // PLANE
    my_z, low = me // PLANE, me % PLANE
    core, x, y = me % 2, low // 2 % 2, low // 4
    rows = hist.shape[0]
    count = rows // seg
    width = hist.shape[1] // nz
    half = width // 2
    block = width // PLANE
    last = nz - 1
    far = nz - 2
    partner = me + 1 - 2 * core
    x_peer, y_peer = me + 2 - 4 * x, me + 4 - 8 * y
    diagonal = me + 2 - 4 * x + 4 - 8 * y
    near = (y_peer, diagonal, x_peer)
    steps = [(i, h) for h in range(2) for i in range(last)] + [(last, 0), (last, 1)]

    def level(i):
        return me + (flip(my_z, last - i) - my_z) * PLANE

    def cols(i, h, dev):
        row = dev % PLANE // 4
        base = flip(dev // PLANE, last - i) * width + ((row + 1 + h) % 2) * half
        return pl.ds(pl.multiple_of(base, half), half)

    def lanes(h):
        return pl.ds(h * half, half)

    def remote(src, dst, send, recv, dev):
        return pltpu.make_async_remote_copy(
            src_ref=src, dst_ref=dst, send_sem=send, recv_sem=recv, device_id=(dev,), device_id_type=MESH
        )

    has_next, has_prev = me < n - 1, me > 0
    outer = me + 2 * core - 1
    has_outer = (outer >= 0) & (outer < n)
    up = has_next & (low == PLANE - 1)
    down = has_prev & (low == 0)
    beside = [partner, x_peer, x_peer + 1 - 2 * core, y_peer, y_peer + 1 - 2 * core]
    over = [me + PLANE, partner + PLANE]
    under = [me - PLANE, partner - PLANE]
    has_over, has_under = my_z < nz - 1, my_z > 0
    met = len(beside) + jnp.where(has_over, len(over), 0) + jnp.where(has_under, len(under), 0)

    def greet(sem):
        def tell(devices):
            for dev in devices:
                pl.semaphore_signal(sem, inc=1, device_id=(dev,), device_id_type=MESH)

        tell(beside)
        pl.when(has_over)(lambda: tell(over))
        pl.when(has_under)(lambda: tell(under))

    barrier = pltpu.get_barrier_semaphore()

    @pl.when(has_outer)
    def _():
        pl.semaphore_signal(barrier, inc=1, device_id=(outer,), device_id_type=MESH)

    greet(barrier)

    constants = pltpu.make_async_copy(tables_h, tables, small_sem.at[0])
    constants.start()
    for i in range(nz):
        for h in range(2):
            for k, src in enumerate((hist, taps)):
                pltpu.make_async_copy(src.at[:, cols(i, h, me)], both_v.at[i, k, :, lanes(h)], load_sem.at[i]).start()
    for k, src in enumerate((self_taps_h, fresh_h, gate_h)):
        pltpu.make_async_copy(src, rows_v.at[k], small_sem.at[1]).start()

    with scope("barrier"):
        pl.semaphore_wait(barrier, met + jnp.where(has_outer, 1, 0))
    greet(ready.at[0])

    def taps_copy(i, h, dev):
        return remote(
            taps.at[pl.ds(rows - seg, seg), cols(i, h, dev)], halo_v.at[i, 0, :, lanes(h)], t_s, halo_r.at[2 * i + h], dev
        )

    def hist_copy(i, h, dev):
        return remote(
            hist.at[pl.ds(0, seg), cols(i, h, dev)], halo_v.at[i, 1, :, lanes(h)], h_s, halo_r.at[2 * i + h], dev
        )

    def send_halo(k, forward_when, back_when):
        i, h = steps[k]

        @pl.when(forward_when)
        def _():
            taps_copy(i, h, me + 1).start()

        @pl.when(back_when)
        def _():
            hist_copy(i, h, me - 1).start()

    for k in range(len(steps)):
        if k < AHEAD:
            send_halo(k, has_next, has_prev)
        else:
            send_halo(k, has_next & ~up, has_prev & ~down)

    def further(stage):
        with scope(f"ready{stage}"):
            pl.semaphore_wait(ready.at[stage], met)
        if stage + 1 < nz - 1:
            greet(ready.at[stage + 1])

    fh, fl, gh, gl = (slice(k, k + r) for k, r in ((0, 2 * seg), (2 * seg, 2 * seg), (4 * seg, seg), (5 * seg, seg)))

    def forward(value):
        both = jnp.concatenate(split(value), axis=0)
        spec = jnp.dot(tables[fh], both, preferred_element_type=F32) + jnp.dot(
            tables[fl], both, preferred_element_type=F32
        )
        return spec[:seg], spec[seg:]

    def keep(ref, i, spec):
        ref[i, :seg], ref[i, seg:] = spec

    def held(ref, i, at):
        return ref[i, :seg, at], ref[i, seg:, at]

    @pl.when(me == 0)
    def _():
        halo_v[:, 0] = jnp.zeros_like(halo_v[:, 0])

    @pl.when(me == n - 1)
    def _():
        halo_v[:, 1] = jnp.zeros_like(halo_v[:, 1])

    constants.wait()

    def local(i):
        pltpu.make_async_copy(both_v.at[i], both_v.at[i], load_sem.at[i]).wait()
        with scope(f"local{i}"):
            hs = [forward(both_v[i, 0, pl.ds(a * seg, seg)]) for a in range(count)]
            ts = [forward(both_v[i, 1, pl.ds(a * seg, seg)]) for a in range(count)]
            first, second = local_products(hs, ts)
            keep(sh0, i, hs[0])
            keep(sh1, i, hs[1])
            keep(st1, i, ts[-2])
            keep(q0, i, first)
            keep(q1, i, second)

    contract = (((1,), (1,)), ((), ()))

    def dot_t(a, b):
        return lax.dot_general(a, b, contract, preferred_element_type=F32)

    def own_part():
        pltpu.make_async_copy(rows_v, rows_v, small_sem.at[1]).wait()
        s, f = rows_v[0], rows_v[1]
        both = jnp.concatenate(
            split(jnp.concatenate([f[:, :seg], f[:, seg:], s[:, :seg], s[:, seg:]], axis=0)), axis=1
        )
        spec = dot_t(both, tables[fh]) + dot_t(both, tables[fl])
        quads = [
            (spec[k * block : (k + 1) * block, :seg], spec[k * block : (k + 1) * block, seg:]) for k in range(4)
        ]
        a, b = own_products(*quads)
        high, low_half = split(
            jnp.concatenate([jnp.concatenate(a, axis=1), jnp.concatenate(b, axis=1)], axis=0)
        )
        res = dot_t(high, tables[gh]) + dot_t(low_half, tables[gh]) + dot_t(high, tables[gl])
        return jnp.concatenate([res[:block], res[block:]], axis=1)

    def inverse(spec):
        hi, lo = split(jnp.concatenate(spec, axis=0))
        return (
            jnp.dot(tables[gh], hi, preferred_element_type=F32)
            + jnp.dot(tables[gh], lo, preferred_element_type=F32)
            + jnp.dot(tables[gl], hi, preferred_element_type=F32)
        ).T

    def chip_copy(i, h):
        k = 2 * i + h
        return remote(parts.at[k, 1 - core], d_recv.at[k], d_s, d_r.at[k], partner)

    def y_copy(i):
        return remote(y_send.at[i], y_recv.at[i], y_s, y_r.at[i], y_peer)

    def w_copy(i, j):
        dev = level(i) + j * (2 - 4 * x)
        place = x + j * (1 - 2 * x)
        return remote(w_send.at[i, place], final.at[3 + 2 * i + j], w_s, final_r, dev)

    def v_copy():
        return remote(v_send, v_recv, v_s, v_r, level(far))

    def near_copy(j):
        src = sums.at[0, x] if j == 0 else sums.at[j - 1, 1 - x]
        return remote(src, final.at[j], n_s, final_r, near[j])

    def compute(i, h):
        with scope(f"halo{i}{h}"):
            @pl.when(has_prev & has_next)
            def _():
                both = halo_v.at[i, :, :, lanes(h)]
                remote(both, both, t_s, halo_r.at[2 * i + h], me).wait_recv()

            @pl.when(~has_next)
            def _():
                taps_copy(i, h, me).wait_recv()

            @pl.when(~has_prev)
            def _():
                hist_copy(i, h, me).wait_recv()

        at_step = steps.index((i, h))
        if at_step + AHEAD < len(steps):
            send_halo(at_step + AHEAD, up, down)

        with scope(f"comp{i}{h}"):
            at = lanes(h)
            both = halo_products(
                held(q0, i, at), held(q1, i, at), held(sh0, i, at), held(sh1, i, at), held(st1, i, at),
                forward(halo_v[i, 0, :, at]), forward(halo_v[i, 1, :, at]),
            )
            for side, spec in enumerate(both):
                res = inverse(spec)
                for k in range(res.shape[0] // block):
                    parts[2 * i + h, k % 2, k // 2, :, pl.ds(side * seg, seg)] = res[k * block : (k + 1) * block]
            chip_copy(i, h).start()

    def chip_sum(i, h):
        with scope(f"chip{i}{h}"):
            chip_copy(i, h).wait_recv()
        return parts[2 * i + h, core] + d_recv[2 * i + h]

    def route_y(i):
        y_send[i] = chip_sum(i, 0)
        y_copy(i).start()

    def route_w(i):
        value = chip_sum(i, 1)
        if i < far:
            with scope(f"y{i}"):
                y_copy(i).wait_recv()
            value = value + y_recv[i]
        w_send[i] = value
        for j in (1, 0):
            w_copy(i, j).start()

    def route_v():
        v_send[...] = chip_sum(far, 0)
        v_copy().start()

    def spread():
        value = chip_sum(last, 0)
        with scope("v"):
            v_copy().wait_recv()
        sums[0] = value + v_recv[...]
        near_copy(0).start()
        near_copy(1).start()

    def finish():
        sums[1] = chip_sum(last, 1)
        near_copy(2).start()

    for i in range(nz):
        local(i)
        if i % 2:
            further(i // 2)
    own = own_part()
    compute(0, 0)
    compute(1, 0)
    for stage in range(nz // 2, nz - 1):
        further(stage)
    route_y(0)
    for i in range(2, last):
        compute(i, 0)
        route_y(i - 1)
    compute(0, 1)
    route_v()
    for i in range(1, last):
        compute(i, 1)
        if i < far:
            route_w(i - 1)
    compute(last, 0)
    route_w(far)
    compute(last, 1)
    route_w(far - 1)
    spread()
    finish()
    total = sums[1, x] + own
    with scope("final"):
        remote(final, final, n_s, final_r, me).wait_recv()
    for k in range(final.shape[0]):
        total = total + final[k]
    out[...] = rows_v[2] * total

    with scope("sends"):
        @pl.when(has_next)
        def _():
            remote(halo_v.at[:, 0], halo_v.at[:, 0], t_s, final_r, me).wait_send()

        @pl.when(has_prev)
        def _():
            remote(halo_v.at[:, 1], halo_v.at[:, 1], h_s, final_r, me).wait_send()

        three = final.at[pl.ds(0, 3)]
        for src, sem in ((d_recv, d_s), (y_send, y_s), (w_send, w_s), (v_send, v_s), (three, n_s)):
            remote(src, src, sem, final_r, me).wait_send()


def kernel_body(history, taps, self_taps, fresh, gate):
    n = lax.axis_size(AXIS)
    rows, channels = history.shape
    block, new_len = fresh.shape
    seg = new_len // 2
    nz = n // PLANE
    width = channels // nz
    fh, fl = halves(dft_matrix(seg))
    gh, gl = halves(dft_matrix(seg).T / seg)
    tables = np.concatenate([np.concatenate([fh, fh], axis=1), np.concatenate([fl, fl], axis=1), gh, gl], axis=0)
    vmem = pl.BlockSpec(memory_space=pltpu.VMEM)
    hbm = pl.BlockSpec(memory_space=pl.ANY)
    dma = pltpu.SemaphoreType.DMA
    spec = pltpu.VMEM((nz, 2 * seg, width), F32)
    far = nz - 2

    def pairs(*lead):
        return pltpu.VMEM((*lead, 2, block, new_len), F32)

    return pl.pallas_call(
        lambda *refs: kernel(n, seg, *refs),
        out_shape=pltpu.VMEM(fresh.shape, F32),
        in_specs=[hbm] * 6,
        out_specs=vmem,
        scratch_shapes=[
            pltpu.VMEM((3, block, new_len), F32),
            pltpu.VMEM(tables.shape, BF16),
            pltpu.VMEM((nz, 2, rows, width), F32),
            pltpu.VMEM((nz, 2, seg, width), F32),
            spec, spec, spec, spec, spec,
            pairs(2 * nz, 2), pairs(2 * nz),
            pairs(far), pairs(far), pairs(far + 1),
            pairs(), pairs(),
            pairs(2),
            pltpu.VMEM((3 + 2 * (far + 1), block, new_len), F32),
            pltpu.SemaphoreType.REGULAR((nz - 1,)),
            dma((2,)), dma((nz,)),
            dma, dma, dma((2 * nz,)),
            dma, dma((2 * nz,)),
            dma, dma((far,)),
            dma,
            dma, dma,
            dma, dma,
        ],
        compiler_params=pltpu.CompilerParams(collective_id=0, has_side_effects=True),
        name="hyena",
    )(history, taps, self_taps, fresh, gate, jnp.asarray(tables))


def solution(mesh):
    n = mesh.shape[AXIS]

    def body(history, taps, self_taps, fresh, gate):
        channels = history.shape[1]
        block = fresh.shape[0]
        planes = n // PLANE
        fits = n % PLANE == 0 and planes >= 4 and planes & (planes - 1) == 0 and block % 32 == 0
        chosen = kernel_body if fits and channels == block * n else plain_body
        return chosen(history, taps, self_taps, fresh, gate)

    spec = P(AXIS, None)
    return jax.shard_map(body, mesh=mesh, in_specs=(spec,) * 5, out_specs=spec, check_vma=False)
```

time: 26.2 us -> 24.1 us (0.920)
  Pallas kernels: 25.5 us -> 23.4 us
    pallas_call x1, Pallas kernels: 25.5 us -> 23.4 us  [kernel_body(): pl.pallas_call(lambda *refs: kernel(n, seg, *refs), out_shape=pltpu.VMEM(...]
where the time goes in v2:
time: 24.1 us; the launch traced here: 24 us
  Pallas kernels  23.4 us (97%)
  local copies, waits for them, and re-layouts  0.62 us (3%)
    pallas_call x1, Pallas kernels, kernel_body(): pl.pallas_call(lambda *refs: kernel(n, seg, *refs), out_shape=pltpu.VMEM(...  23.4 us
    unnamed x1, local copies, waits for them, and re-layouts  0.62 us

profile of v2, /device:TPU:0, one launch (start us, length us, event | category | flops | bytes accessed | tf_op | source)
XLA Modules:
  0.0 24.0 jit_solution(7762081276935547841)
XLA Ops:
  0.0 23.4 %hyena.1 = f32[32,256]{1,0:T(8,128)S(1)} custom-call(f32[384,1024]{1,0:T(8,128)} %refs_0_.1, f32[384,1024]{1,0:T(8,128)} %refs_1_.1, f32[32,256]{1,0:T(8,128)} %refs_2_.1, f32[32,256]{1,0:T(8,128)} %refs_3_.1, f32[32,256]{1,0:T(8,128)} %refs_4_.1, bf16[768,256]{1,0:T(8,128)(2,1)} %constant.2.clone.refs_5_), custom_call_target="tpu_custom_call" | custom-call | tf_op jit(solution)/shard_map/hyena/pallas_call | solution.py:444
  23.4 0.6 %copy.8 = f32[32,256]{1,0:T(8,128)} copy(f32[32,256]{1,0:T(8,128)S(1)} %hyena.1) | data formatting | bytes 65536

commit v3 on v2

--- a/solution.py
+++ b/solution.py
@@ -134,13 +134,29 @@
     near = (y_peer, diagonal, x_peer)
     steps = [(i, h) for h in range(2) for i in range(last)] + [(last, 0), (last, 1)]
 
+    def plane(i, z):
+        straight = flip(z, last - i)
+        if i >= far:
+            return straight
+        low_first = flip(z, last - i // 2 * 2) // 2 * 2 + i % 2
+        return jnp.where(z >= nz // 2, low_first, straight)
+
     def level(i):
-        return me + (flip(my_z, last - i) - my_z) * PLANE
+        return me + (plane(i, my_z) - my_z) * PLANE
 
     def cols(i, h, dev):
-        row = dev % PLANE // 4
-        base = flip(dev // PLANE, last - i) * width + ((row + 1 + h) % 2) * half
+        row = (dev % PLANE // 4 + 1 + h) % 2
+        if i == last:
+            row = jnp.where(dev < PLANE, h, row)
+        base = plane(i, dev // PLANE) * width + row * half
         return pl.ds(pl.multiple_of(base, half), half)
+
+    def differ(a, b):
+        value, bit = 0, 1
+        while bit < nz:
+            value = value + bit * ((a // bit + b // bit) % 2)
+            bit *= 2
+        return value
 
     def lanes(h):
         return pl.ds(h * half, half)
@@ -301,7 +317,8 @@
     def w_copy(i, j):
         dev = level(i) + j * (2 - 4 * x)
         place = x + j * (1 - 2 * x)
-        return remote(w_send.at[i, place], final.at[3 + 2 * i + j], w_s, final_r, dev)
+        slot = 3 + 2 * (last - differ(my_z, plane(i, my_z))) + j
+        return remote(w_send.at[i, place], final.at[slot], w_s, final_r, dev)
 
     def v_copy():
         return remote(v_send, v_recv, v_s, v_r, level(far))
@@ -342,7 +359,7 @@
             chip_copy(i, h).start()
 
     def chip_sum(i, h):
-        with scope(f"chip{i}{h}"):
+        with scope(f"chip{i}{h if isinstance(h, int) else ''}"):
             chip_copy(i, h).wait_recv()
         return parts[2 * i + h, core] + d_recv[2 * i + h]
 
@@ -364,8 +381,10 @@
         v_send[...] = chip_sum(far, 0)
         v_copy().start()
 
+    swap = me < PLANE // 2
+
     def spread():
-        value = chip_sum(last, 0)
+        value = chip_sum(last, jnp.where(swap, 1, 0))
         with scope("v"):
             v_copy().wait_recv()
         sums[0] = value + v_recv[...]
@@ -373,7 +392,7 @@
         near_copy(1).start()
 
     def finish():
-        sums[1] = chip_sum(last, 1)
+        sums[1] = chip_sum(last, jnp.where(swap, 0, 1))
         near_copy(2).start()
 
     for i in range(nz):
@@ -398,9 +417,10 @@
     compute(last, 0)
     route_w(far)
     compute(last, 1)
+    pl.when(swap)(finish)
     route_w(far - 1)
     spread()
-    finish()
+    pl.when(~swap)(finish)
     total = sums[1, x] + own
     with scope("final"):
         remote(final, final, n_s, final_r, me).wait_recv()

time: 24.1 us -> 23.2 us (0.963)
  Pallas kernels: 23.4 us -> 22.3 us
    pallas_call x1, Pallas kernels: 23.4 us -> 22.3 us  [kernel_body(): pl.pallas_call(lambda *refs: kernel(n, seg, *refs), out_shape=pltpu.VMEM(...]
where the time goes in v3:
time: 23.2 us; the launch traced here: 22.9 us
  Pallas kernels  22.3 us (96%)
  local copies, waits for them, and re-layouts  0.62 us (3%)
    pallas_call x1, Pallas kernels, kernel_body(): pl.pallas_call(lambda *refs: kernel(n, seg, *refs), out_shape=pltpu.VMEM(...  22.3 us
    unnamed x1, local copies, waits for them, and re-layouts  0.62 us

profile of v3, /device:TPU:0, one launch (start us, length us, event | category | flops | bytes accessed | tf_op | source)
XLA Modules:
  0.0 22.9 jit_solution(5412755875949824621)
XLA Ops:
  0.0 22.3 %hyena.1 = f32[32,256]{1,0:T(8,128)S(1)} custom-call(f32[384,1024]{1,0:T(8,128)} %refs_0_.1, f32[384,1024]{1,0:T(8,128)} %refs_1_.1, f32[32,256]{1,0:T(8,128)} %refs_2_.1, f32[32,256]{1,0:T(8,128)} %refs_3_.1, f32[32,256]{1,0:T(8,128)} %refs_4_.1, bf16[768,256]{1,0:T(8,128)(2,1)} %constant.2.clone.refs_5_), custom_call_target="tpu_custom_call" | custom-call | tf_op jit(solution)/shard_map/hyena/pallas_call | solution.py:464
  22.3 0.6 %copy.8 = f32[32,256]{1,0:T(8,128)} copy(f32[32,256]{1,0:T(8,128)S(1)} %hyena.1) | data formatting | bytes 65536

commit v4 on v3

--- a/solution.py
+++ b/solution.py
@@ -116,7 +116,7 @@
 def kernel(n, seg, hist, taps, self_taps_h, fresh_h, gate_h, tables_h, out,
            rows_v, tables, both_v, halo_v, sh0, sh1, st1, q0, q1,
            parts, d_recv, y_send, y_recv, w_send, v_send, v_recv, sums, final,
-           ready, small_sem, load_sem, t_s, h_s, halo_r, d_s, d_r, y_s, y_r, w_s, v_s, v_r, n_s, final_r):
+           ready, small_sem, load_sem, edge_sem, t_s, h_s, halo_r, d_s, d_r, y_s, y_r, w_s, v_s, v_r, n_s, final_r):
     me = lax.axis_index(AXIS)
     nz = n // PLANE
     my_z, low = me // PLANE, me % PLANE
@@ -144,11 +144,12 @@
     def level(i):
         return me + (plane(i, my_z) - my_z) * PLANE
 
+    def half_row(i, h, dev):
+        row = (dev % PLANE // 4 + 1 + h) % 2
+        return jnp.where(dev < PLANE, h, row) if i == last else row
+
     def cols(i, h, dev):
-        row = (dev % PLANE // 4 + 1 + h) % 2
-        if i == last:
-            row = jnp.where(dev < PLANE, h, row)
-        base = plane(i, dev // PLANE) * width + row * half
+        base = plane(i, dev // PLANE) * width + half_row(i, h, dev) * half
         return pl.ds(pl.multiple_of(base, half), half)
 
     def differ(a, b):
@@ -196,26 +197,46 @@
 
     constants = pltpu.make_async_copy(tables_h, tables, small_sem.at[0])
     constants.start()
+
+    def load(i, h, k, start, length, sem):
+        span = pl.ds(start, length)
+        pltpu.make_async_copy((hist, taps)[k].at[span, cols(i, h, me)], both_v.at[i, k, span, lanes(h)], sem).start()
+
+    rest = rows - seg
     for i in range(nz):
         for h in range(2):
-            for k, src in enumerate((hist, taps)):
-                pltpu.make_async_copy(src.at[:, cols(i, h, me)], both_v.at[i, k, :, lanes(h)], load_sem.at[i]).start()
+            load(i, h, 0, 0, seg, edge_sem)
+            load(i, h, 1, rest, seg, edge_sem)
+    for i in range(nz):
+        for h in range(2):
+            load(i, h, 0, seg, rest, load_sem.at[i])
+            load(i, h, 1, 0, rest, load_sem.at[i])
     for k, src in enumerate((self_taps_h, fresh_h, gate_h)):
         pltpu.make_async_copy(src, rows_v.at[k], small_sem.at[1]).start()
 
     with scope("barrier"):
         pl.semaphore_wait(barrier, met + jnp.where(has_outer, 1, 0))
     greet(ready.at[0])
+    pltpu.make_async_copy(halo_v, halo_v, edge_sem).wait()
+
+    def mine(i, dev):
+        goal = plane(i, dev // PLANE)
+        mask = differ(my_z, goal)
+        straight = last - mask
+        return jnp.where((my_z >= nz // 2) & (mask >= 2), straight // 2 * 2 + goal % 2, straight)
+
+    def spot(i, h, dev):
+        row = half_row(i, h, dev)
+        place = jnp.where((me < PLANE) & (plane(i, dev // PLANE) == my_z), row, (row + y + 1) % 2)
+        return pl.ds(pl.multiple_of(place * half, half), half)
 
     def taps_copy(i, h, dev):
-        return remote(
-            taps.at[pl.ds(rows - seg, seg), cols(i, h, dev)], halo_v.at[i, 0, :, lanes(h)], t_s, halo_r.at[2 * i + h], dev
-        )
+        src = both_v.at[mine(i, dev), 1, pl.ds(rows - seg, seg), spot(i, h, dev)]
+        return remote(src, halo_v.at[i, 0, :, lanes(h)], t_s, halo_r.at[2 * i + h], dev)
 
     def hist_copy(i, h, dev):
-        return remote(
-            hist.at[pl.ds(0, seg), cols(i, h, dev)], halo_v.at[i, 1, :, lanes(h)], h_s, halo_r.at[2 * i + h], dev
-        )
+        src = both_v.at[mine(i, dev), 0, pl.ds(0, seg), spot(i, h, dev)]
+        return remote(src, halo_v.at[i, 1, :, lanes(h)], h_s, halo_r.at[2 * i + h], dev)
 
     def send_halo(k, forward_when, back_when):
         i, h = steps[k]
@@ -266,7 +287,8 @@
     constants.wait()
 
     def local(i):
-        pltpu.make_async_copy(both_v.at[i], both_v.at[i], load_sem.at[i]).wait()
+        some = both_v.at[i, :, pl.ds(0, rest)]
+        pltpu.make_async_copy(some, some, load_sem.at[i]).wait()
         with scope(f"local{i}"):
             hs = [forward(both_v[i, 0, pl.ds(a * seg, seg)]) for a in range(count)]
             ts = [forward(both_v[i, 1, pl.ds(a * seg, seg)]) for a in range(count)]
@@ -399,7 +421,6 @@
         local(i)
         if i % 2:
             further(i // 2)
-    own = own_part()
     compute(0, 0)
     compute(1, 0)
     for stage in range(nz // 2, nz - 1):
@@ -421,6 +442,7 @@
     route_w(far - 1)
     spread()
     pl.when(~swap)(finish)
+    own = own_part()
     total = sums[1, x] + own
     with scope("final"):
         remote(final, final, n_s, final_r, me).wait_recv()
@@ -478,7 +500,7 @@
             pairs(2),
             pltpu.VMEM((3 + 2 * (far + 1), block, new_len), F32),
             pltpu.SemaphoreType.REGULAR((nz - 1,)),
-            dma((2,)), dma((nz,)),
+            dma((2,)), dma((nz,)), dma,
             dma, dma, dma((2 * nz,)),
             dma, dma((2 * nz,)),
             dma, dma((far,)),

time: 23.2 us -> 22.9 us (0.987)
  no operation moved by 1% of the time
where the time goes in v4:
time: 22.9 us; the launch traced here: 22.7 us
  Pallas kernels  22.1 us (97%)
  local copies, waits for them, and re-layouts  0.62 us (3%)
    pallas_call x1, Pallas kernels, kernel_body(): pl.pallas_call(lambda *refs: kernel(n, seg, *refs), out_shape=pltpu.VMEM(...  22.1 us
    unnamed x1, local copies, waits for them, and re-layouts  0.62 us

profile of v4, /device:TPU:0, one launch (start us, length us, event | category | flops | bytes accessed | tf_op | source)
XLA Modules:
  0.0 22.7 jit_solution(12742744463698551351)
XLA Ops:
  0.0 22.1 %hyena.1 = f32[32,256]{1,0:T(8,128)S(1)} custom-call(f32[384,1024]{1,0:T(8,128)} %refs_0_.1, f32[384,1024]{1,0:T(8,128)} %refs_1_.1, f32[32,256]{1,0:T(8,128)} %refs_2_.1, f32[32,256]{1,0:T(8,128)} %refs_3_.1, f32[32,256]{1,0:T(8,128)} %refs_4_.1, bf16[768,256]{1,0:T(8,128)(2,1)} %constant.2.clone.refs_5_), custom_call_target="tpu_custom_call" | custom-call | tf_op jit(solution)/shard_map/hyena/pallas_call | solution.py:486
  22.1 0.6 %copy.8 = f32[32,256]{1,0:T(8,128)} copy(f32[32,256]{1,0:T(8,128)S(1)} %hyena.1) | data formatting | bytes 65536

commit v5 on v4

--- a/solution.py
+++ b/solution.py
@@ -437,9 +437,9 @@
             route_w(i - 1)
     compute(last, 0)
     route_w(far)
+    route_w(far - 1)
     compute(last, 1)
     pl.when(swap)(finish)
-    route_w(far - 1)
     spread()
     pl.when(~swap)(finish)
     own = own_part()

time: 22.9 us -> 22.9 us (level)
  no operation moved by 1% of the time
where the time goes in v5:
time: 22.9 us; the launch traced here: 22.7 us
  Pallas kernels  22.1 us (97%)
  local copies, waits for them, and re-layouts  0.62 us (3%)
    pallas_call x1, Pallas kernels, kernel_body(): pl.pallas_call(lambda *refs: kernel(n, seg, *refs), out_shape=pltpu.VMEM(...  22.1 us
    unnamed x1, local copies, waits for them, and re-layouts  0.62 us

profile of v5, /device:TPU:0, one launch (start us, length us, event | category | flops | bytes accessed | tf_op | source)
XLA Modules:
  0.0 22.7 jit_solution(11497575159983955038)
XLA Ops:
  0.0 22.1 %hyena.1 = f32[32,256]{1,0:T(8,128)S(1)} custom-call(f32[384,1024]{1,0:T(8,128)} %refs_0_.1, f32[384,1024]{1,0:T(8,128)} %refs_1_.1, f32[32,256]{1,0:T(8,128)} %refs_2_.1, f32[32,256]{1,0:T(8,128)} %refs_3_.1, f32[32,256]{1,0:T(8,128)} %refs_4_.1, bf16[768,256]{1,0:T(8,128)(2,1)} %constant.2.clone.refs_5_), custom_call_target="tpu_custom_call" | custom-call | tf_op jit(solution)/shard_map/hyena/pallas_call | solution.py:486
  22.1 0.6 %copy.8 = f32[32,256]{1,0:T(8,128)} copy(f32[32,256]{1,0:T(8,128)S(1)} %hyena.1) | data formatting | bytes 65536
